TPU v7x, 32 devices: a whole 2x2x4 slice. The times are simulated.
32 devices in a mesh: dp: 4 (over x, core), expert: 8 (over z, y).
Axes of the slice: x: 2, y: 2, z: 4, core: 2. Of those that a mesh axis runs over, the one named last changes fastest.
Arguments:
- tokens: bfloat16 [4096, 2048], P(('dp', 'expert')), may hold values from -6 to 6
- norm_gain: bfloat16 [2048], replicated, may hold values from 0.099609375 to 1.8984375
- router_weight: bfloat16 [2048, 8], replicated, may hold values from -0.1875 to 0.1875
- w_gate: bfloat16 [8, 2048, 5120], P('expert', None, 'dp'), may hold values from -0.125 to 0.125
- w_up: bfloat16 [8, 2048, 5120], P('expert', None, 'dp'), may hold values from -0.125 to 0.125
- w_down: bfloat16 [8, 5120, 2048], P('expert', 'dp'), may hold values from -0.078125 to 0.078125
- selected: int32 [8, 896], replicated, may hold values from 0 to 4095, as said below
Outputs:
- combined: bfloat16 [4096, 2048], P(('dp', 'expert'))
Inputs may be any that keep to these rules, and one draw needn't show every extreme that they name: `selected`: each row holds 896 distinct token indices in ascending order. Of one row's indices at most 64 fall among one device's 128 tokens and at most 336 among the tokens of one index of dp; every row reaches both bounds.
All inputs are finite; a program needn't handle non-finite values.
Results may differ from a plain program's by a relative error of at most 0.0072.
Values may be sent and summed in bfloat16 or wider, within the bound.
A program may use at most 128 MiB of HBM per device.

v0:
```python
import jax
import jax.numpy as jnp
from jax import lax
from jax.sharding import PartitionSpec as P


def run_rank(labels):
    length = labels.shape[0]
    places = jnp.arange(length, dtype=jnp.int32)
    changes = jnp.concatenate([jnp.ones((1,), jnp.bool_), labels[1:] != labels[:-1]])
    starts = jnp.where(changes, places, 0)
    return places - lax.cummax(starts, axis=0)


def per_device(tokens, norm_gain, router_weight, w_gate, w_up, w_down, selected):
    dp_count = lax.axis_size("dp")
    expert_count = lax.axis_size("expert")
    tok_rows, model_width = tokens.shape
    experts, capacity = selected.shape
    peak_slots = 4 * tok_rows // experts
    dp_index = lax.axis_index("dp")
    expert_index = lax.axis_index("expert")
    source = dp_index * expert_count + expert_index
    activations = tokens.astype(jnp.float32)
    mean_square = jnp.mean(activations * activations, axis=1, keepdims=True)
    normed = (activations * lax.rsqrt(mean_square + 1e-06) * norm_gain.astype(jnp.float32)).astype(
        jnp.bfloat16
    )
    gate_probs = jax.nn.sigmoid(jnp.dot(normed, router_weight, preferred_element_type=jnp.float32))
    lowest = source * tok_rows
    below_count = jnp.sum((selected < lowest).astype(jnp.int32), axis=1)
    upto_count = jnp.sum((selected < lowest + tok_rows).astype(jnp.int32), axis=1)
    slot_range = jnp.arange(peak_slots, dtype=jnp.int32)
    places = jnp.clip(below_count[:, None] + slot_range[None, :], 0, capacity - 1)
    is_valid = slot_range[None, :] < (upto_count - below_count)[:, None]
    local_index = jnp.where(is_valid, jnp.take_along_axis(selected, places, axis=1) - lowest, 0)
    outgoing = jnp.where(is_valid[:, :, None], normed[local_index], 0)
    slot_gate = jnp.where(is_valid, jnp.take_along_axis(gate_probs.T, local_index, axis=1), 0.0)
    received = lax.all_to_all(outgoing, "expert", split_axis=0, concat_axis=0, tiled=True)
    expert_row = lax.dynamic_index_in_dim(selected, expert_index, 0, keepdims=False)
    owners = expert_row // tok_rows
    ranks = run_rank(owners)
    block_rows = expert_count * tok_rows
    row_room = 3 * capacity // (2 * dp_count)
    row_first = jnp.sum((expert_row < dp_index * block_rows).astype(jnp.int32))
    row_last = jnp.sum((expert_row < (dp_index + 1) * block_rows).astype(jnp.int32))
    wanted = row_first + jnp.arange(row_room, dtype=jnp.int32)
    is_usable = wanted < row_last
    clipped = jnp.clip(wanted, 0, capacity - 1)
    sender = owners[clipped] - dp_index * expert_count
    lookup = jnp.clip(sender * peak_slots + ranks[clipped], 0, expert_count * peak_slots - 1)
    packed = jnp.where(is_usable[:, None], received.reshape(-1, model_width)[lookup], 0)
    everything = lax.all_gather(packed, "dp", axis=0, tiled=True)
    row_owner = owners // expert_count
    row_index = row_owner * row_room + run_rank(row_owner)
    expert_rows = everything[row_index]
    gate_part = jnp.dot(expert_rows, w_gate[0], preferred_element_type=jnp.float32)
    up_part = jnp.dot(expert_rows, w_up[0], preferred_element_type=jnp.float32)
    hidden = (jax.nn.gelu(gate_part, approximate=True) * up_part).astype(jnp.bfloat16)
    partial_value = jnp.dot(hidden, w_down[0], preferred_element_type=jnp.float32)
    term_rows = (
        jnp.zeros((dp_count * row_room, model_width), jnp.float32).at[row_index].set(partial_value)
    )
    own_part = lax.psum_scatter(term_rows, "dp", scatter_dimension=0, tiled=True).astype(
        jnp.bfloat16
    )
    group_sources = dp_index * expert_count + jnp.arange(expert_count, dtype=jnp.int32)
    firsts = jnp.sum(
        (expert_row[None, :] < group_sources[:, None] * tok_rows).astype(jnp.int32), axis=1
    )
    lasts = jnp.sum(
        (expert_row[None, :] < (group_sources[:, None] + 1) * tok_rows).astype(jnp.int32), axis=1
    )
    offsets = jnp.clip(firsts[:, None] + slot_range[None, :] - row_first, 0, row_room - 1)
    fitting = slot_range[None, :] < (lasts - firsts)[:, None]
    returning = jnp.where(fitting[:, :, None], own_part[offsets], 0)
    arrived = lax.all_to_all(returning, "expert", split_axis=0, concat_axis=0, tiled=True)
    token_range = jnp.arange(tok_rows, dtype=jnp.int32)
    mixing = jnp.where(
        local_index.reshape(1, -1) == token_range[:, None], slot_gate.reshape(1, -1), 0.0
    )
    combined = jnp.dot(
        mixing,
        arrived.reshape(-1, model_width).astype(jnp.float32),
        precision=lax.Precision.HIGHEST,
    )
    return combined.astype(jnp.bfloat16)


def solution(mesh):
    in_specs = (
        P(("dp", "expert"), None),
        P(),
        P(),
        P("expert", None, "dp"),
        P("expert", None, "dp"),
        P("expert", "dp", None),
        P(),
    )
    out_specs = P(("dp", "expert"), None)
    return jax.shard_map(
        per_device, mesh=mesh, in_specs=in_specs, out_specs=out_specs, check_vma=False
    )
```

profile of v0, /device:TPU:0, one launch (start us, length us, event | category | flops | bytes accessed | tf_op | source)
XLA Modules:
  0.0 336.1 jit_solution(5497459514095636806)
XLA Ops:
  6.5 1.3 fusion.23
  7.8 0.9 convert_reduce_fusion.3
  8.8 0.1 shift-left_or_fusion.1
  8.8 0.1 iota_compare_fusion.2
  8.9 0.1 reshape.666
  9.0 4.4 %gather_fusion.6 = s32[512]{0:T(512)S(1)} fusion(s32[8,896]{1,0:T(8,128)} %param.13, s32[512]{0:T(512)S(1)} %reshape.666), kind=kCustom, calls=%fused_computation.6 | custom fusion | bytes 8192 | tf_op jit(solution)/shard_map/jit(take_along_axis)/gather | solution.py:36
  13.4 0.1 gather.34
  13.5 0.1 shift-left_or_fusion
  13.6 0.1 reshape.620
  13.7 0.2 fusion.25
  13.9 2.5 gather_fusion
  16.4 1.6 broadcast_select_fusion
  17.9 7.3 %all-to-all-start = ((bf16[8,64,2048]{2,1,0:T(8,128)(2,1)}), bf16[8,64,2048]{2,1,0:T(8,128)(2,1)S(1)}, u32[]{:S(2)}, u32[]{:S(2)}) async-start(bf16[8,64,2048]{2,1,0:T(8,128)(2,1)} %broadcast_select_fusion), calls=%async_computation | async-start | bytes 4194304 | tf_op jit(solution)/shard_map/all_to_all | solution.py:39
  25.2 0.0 all-gather.2.cloned.1.call-start
  25.3 0.8 dynamic-slice_reduce_fusion
  26.0 0.7 convert_reduce_fusion.4
  26.8 0.7 fusion.45
  27.4 1.9 gather_fusion.1
  29.3 0.1 slice_compare_fusion
  29.4 0.1 slice_compare_fusion.1
  29.5 0.1 fusion.34
  29.5 0.3 reduce-window.24
  29.8 0.1 slice.32
  29.9 0.1 slice_reduce_fusion
  30.0 0.1 bitcast_subtract_fusion
  30.1 1.9 gather_fusion.2
  32.1 1.3 add_compare_fusion
  33.4 40.1 %all-to-all-done = bf16[8,64,2048]{2,1,0:T(8,128)(2,1)S(1)} async-done(((bf16[8,64,2048]{2,1,0:T(8,128)(2,1)}), bf16[8,64,2048]{2,1,0:T(8,128)(2,1)S(1)}, u32[]{:S(2)}, u32[]{:S(2)}) %all-to-all-start) | async-done | bytes 2097184 | tf_op jit(solution)/shard_map/all_to_all | solution.py:39
  73.5 3.0 gather_fusion.3
  76.5 2.6 broadcast_select_fusion.2
  79.1 0.0 all-gather.2.cloned.1.call-update
  79.1 0.0 reduce-scatter.2.cloned.1.call-start
  79.2 0.3 reduce-window.16
  79.5 0.1 slice.28
  79.6 0.1 slice_reduce_fusion.1
  79.7 0.1 maximum_bitcast_fusion
  79.8 0.8 fusion.43
  80.6 39.7 %all-gather.2.cloned.1.call-done = bf16[1344,2048]{1,0:T(8,128)(2,1)} async-done(((bf16[336,2048]{1,0:T(8,128)(2,1)}), bf16[1344,2048]{1,0:T(8,128)(2,1)}) %all-gather.2.cloned.1.call-update) | async-done | bytes 5505040 | tf_op jit(solution)/shard_map/all_gather | solution.py:53
  120.2 12.1 %gather_fusion.4 = bf16[896,2048]{1,0:T(8,128)(2,1)} fusion(bf16[1344,2048]{1,0:T(8,128)(2,1)} %all-gather.2.cloned.1.call-done, s32[1024]{0:T(1024)S(1)} %pad_clamp_fusion.1), kind=kCustom, calls=%fused_computation.4 | custom fusion | bytes 7343616 | tf_op jit(solution)/shard_map/gather | solution.py:56
  132.3 10.5 %fusion.4 = f32[896,1280]{1,0:T(8,128)} fusion(bf16[896,2048]{1,0:T(8,128)(2,1)} %gather_fusion.4, bf16[1,2048,1280]{2,1,0:T(8,128)(2,1)} %param.11), kind=kOutput, calls=%fused_computation.14 | convolution fusion | flops 4697620480 | bytes 13500416 | tf_op jit(solution)/shard_map/dot_general | solution.py:58
  142.9 20.5 %fusion.2 = f32[896,2048]{1,0:T(8,128)} fusion(bf16[1,1280,2048]{2,1,0:T(8,128)(2,1)} %param.12, f32[896,1280]{1,0:T(8,128)} %fusion.4, bf16[896,2048]{1,0:T(8,128)(2,1)} %gather_fusion.4, bf16[1,2048,1280]{2,1,0:T(8,128)(2,1)} %param.10), kind=kOutput, calls=%fused_computation.12 | convolution fusion | flops 9406709760 | bytes 26083328 | tf_op jit(solution)/shard_map/dot_general | solution.py:60
  163.4 14.2 %scatter_custom_fusion = f32[1344,2048]{1,0:T(8,128)} fusion(s32[896]{0:T(1024)S(1)} %fusion.43, f32[896,2048]{1,0:T(8,128)} %fusion.2, f32[]{:T(128)} %constant.65.clone.1), kind=kCustom, calls=%fused_computation.10 | custom fusion | bytes 11010560 | tf_op jit(solution)/shard_map/scatter | solution.py:62
  177.6 0.2 convert_reduce_fusion.1
  177.9 0.7 compare_select_fusion.1
  178.6 0.1 reshape.660
  178.7 0.1 iota_compare_fusion.3
  178.7 86.7 %reduce-scatter.2.cloned.1.call-done = f32[336,2048]{1,0:T(8,128)} async-done(((f32[1344,2048]{1,0:T(8,128)}), f32[336,2048]{1,0:T(8,128)}) %reduce-scatter.2.cloned.1.call-update) | async-done | bytes 2752528 | tf_op jit(solution)/shard_map/reduce_scatter | solution.py:64
  265.4 2.0 convert_element_type.52
  267.4 3.3 gather_fusion.5
  270.7 3.1 broadcast_select_fusion.1
  273.8 5.5 %all-to-all-start.1 = ((bf16[8,64,2048]{2,1,0:T(8,128)(2,1)}), bf16[8,64,2048]{2,1,0:T(8,128)(2,1)S(1)}, u32[]{:S(2)}, u32[]{:S(2)}) async-start(bf16[8,64,2048]{2,1,0:T(8,128)(2,1)} %broadcast_select_fusion.1), calls=%async_computation.2 | async-start | bytes 4194304 | tf_op jit(solution)/shard_map/all_to_all | solution.py:77
  279.3 0.1 lt.252
  279.4 0.1 lt.253
  279.5 0.1 broadcast_reduce_fusion
  279.6 0.1 add.308
  279.7 0.1 reshape.672
  279.7 0.1 add.298
  279.8 0.1 add.299
  279.9 0.1 lt.256
  280.0 0.1 lt.247
  280.1 0.2 fusion.22
  280.3 2.5 gather_fusion.7
  282.9 44.6 %all-to-all-done.1 = bf16[8,64,2048]{2,1,0:T(8,128)(2,1)S(1)} async-done(((bf16[8,64,2048]{2,1,0:T(8,128)(2,1)}), bf16[8,64,2048]{2,1,0:T(8,128)(2,1)S(1)}, u32[]{:S(2)}, u32[]{:S(2)}) %all-to-all-start.1) | async-done | bytes 2097184 | tf_op jit(solution)/shard_map/all_to_all | solution.py:77
  327.4 1.8 convolution_convert_fusion
  (25 shorter events, 0.2 us)
Async XLA Ops:
  6.5 273.5 %copy-start = (bf16[2048,8]{0,1:T(8,128)(2,1)S(1)}, bf16[2048,8]{0,1:T(8,128)(2,1)}, u32[]{:S(2)}) copy-start(bf16[2048,8]{0,1:T(8,128)(2,1)} %param.9) | copy-start | bytes 98308
  6.5 7.1 %copy-start.1 = (bf16[128,2048]{1,0:T(8,128)(2,1)S(1)}, bf16[128,2048]{1,0:T(8,128)(2,1)}, u32[]{:S(2)}) copy-start(bf16[128,2048]{1,0:T(8,128)(2,1)} %param.7) | copy-start | bytes 1572868
  6.5 7.1 %copy-start.2 = (bf16[2048]{0:T(1024)(128)(2,1)S(1)}, bf16[2048]{0:T(1024)(128)(2,1)}, u32[]{:S(2)}) copy-start(bf16[2048]{0:T(1024)(128)(2,1)} %param.8) | copy-start | bytes 12292
  17.9 55.5 %all-to-all-start = ((bf16[8,64,2048]{2,1,0:T(8,128)(2,1)}), bf16[8,64,2048]{2,1,0:T(8,128)(2,1)S(1)}, u32[]{:S(2)}, u32[]{:S(2)}) async-start(bf16[8,64,2048]{2,1,0:T(8,128)(2,1)} %broadcast_select_fusion), calls=%async_computation | async-start | bytes 4194304 | tf_op jit(solution)/shard_map/all_to_all | solution.py:39
  25.2 95.0 %all-gather.2.cloned.1.call-start = ((), (), s32[]{:S(2)}) async-start(), calls=%async_computation.3 | async-start | bytes 6881280 | tf_op jit(solution)/shard_map/all_gather | solution.py:53
  79.1 186.3 %reduce-scatter.2.cloned.1.call-start = ((), (), s32[]{:S(2)}) async-start(), calls=%async_computation.4 | async-start | bytes 13762560 | tf_op jit(solution)/shard_map/reduce_scatter | solution.py:64
  273.8 53.6 %all-to-all-start.1 = ((bf16[8,64,2048]{2,1,0:T(8,128)(2,1)}), bf16[8,64,2048]{2,1,0:T(8,128)(2,1)S(1)}, u32[]{:S(2)}, u32[]{:S(2)}) async-start(bf16[8,64,2048]{2,1,0:T(8,128)(2,1)} %broadcast_select_fusion.1), calls=%async_computation.2 | async-start | bytes 4194304 | tf_op jit(solution)/shard_map/all_to_all | solution.py:77
Sparse Core Ops, SparseCore 0:
  79.3 40.9 all-gather.1
  177.7 87.6 reduce-scatter.1
where the time goes:
time: 337 us; the launch traced here: 336 us
  waiting for transfers between devices  211 us (63%)
  local copies, waits for them, and re-layouts  48 us (14%)
  matrix products  33.1 us (10%)
  other arithmetic  17.5 us (5%)
  between operations  13.6 us (4%)
  starting transfers between devices  12.9 us (4%)
    reduce_scatter x1, waiting for transfers between devices, per_device(): lax.psum_scatter(term_rows, 'dp', scatter_dimension=0, tiled=True)  86.7 us
    all_to_all x1, waiting for transfers between devices, per_device(): lax.all_to_all(returning, 'expert', split_axis=0, concat_axis=0, tiled=True)  44.6 us
    all_to_all x1, waiting for transfers between devices, per_device(): lax.all_to_all(outgoing, 'expert', split_axis=0, concat_axis=0, tiled=True)  40.1 us
    all_gather x1, waiting for transfers between devices, per_device(): everything = lax.all_gather(packed, 'dp', axis=0, tiled=True)  39.7 us
    dot_general x1, matrix products, per_device(): jnp.dot(hidden, w_down[0], preferred_element_type=jnp.float32)  20.5 us
    scatter x1, local copies, waits for them, and re-layouts, per_device(): jnp.zeros((dp_count * row_room, model_width), jnp.float32).at[row_index]  14.2 us
    gather x1, local copies, waits for them, and re-layouts, per_device(): expert_rows = everything[row_index]  12.1 us
    dot_general x1, matrix products, per_device(): up_part = jnp.dot(expert_rows, w_up[0], preferred_element_type=jnp.float32)  10.5 us
  transfers between devices with their start and end apart: 4, of which 4 were waited for; matrix products, arithmetic and copies ran while one was open for 4% of the time, Pallas kernels for 0%

commit v1 on v0

v1 whole, which is shorter than its diff:
```python
import functools

import jax
import jax.numpy as jnp
from jax import lax
from jax.experimental import pallas as pl
from jax.experimental.pallas import tpu as pltpu
from jax.sharding import PartitionSpec as P

MESH = pl.DeviceIdType.MESH
F32 = jnp.float32
BF16 = jnp.bfloat16
CHUNKS_IN = 4
CHUNKS_OUT = 4


def tile_of(width):
    for tile in (256, 128):
        if width % tile == 0:
            return tile
    return width


def greet(experts, chips):
    me = lax.axis_index("expert")
    dp = lax.axis_index("dp")
    chip, core = dp // 2, dp % 2
    barrier = pltpu.get_barrier_semaphore()

    def expert_hello(i, carry):
        pl.semaphore_signal(
            barrier, inc=1, device_id={"expert": (me + i) % experts}, device_id_type=MESH
        )
        return carry

    lax.fori_loop(1, experts, expert_hello, 0)
    pl.semaphore_signal(
        barrier, inc=1, device_id={"dp": 2 * chip + 1 - core}, device_id_type=MESH
    )
    for i in range(1, chips):
        pl.semaphore_signal(
            barrier,
            inc=1,
            device_id={"dp": 2 * ((chip + i) % chips) + core},
            device_id_type=MESH,
        )
    pl.semaphore_wait(barrier, experts - 1 + chips)
    return me, dp, chip, core


def remote(src, dst, send_sem, recv_sem, **where):
    return pltpu.make_async_remote_copy(
        src_ref=src,
        dst_ref=dst,
        send_sem=send_sem,
        recv_sem=recv_sem,
        device_id=where,
        device_id_type=MESH,
    )


def kernel_in(
    experts, chips, chunks,
    normed, pick, pack, wg_hbm, wu_hbm, hidden,
    outgoing, received, rows, wg, wu, acc_g, acc_u,
    w_sem, a_send, a_recv, x_send, s_send, b_recv,
):
    dp_count = 2 * chips
    width = normed.shape[1] // chunks
    slots = outgoing.shape[2]
    room = rows.shape[2]
    ff = wg.shape[1]
    tile = tile_of(ff)

    def weights(k):
        part = pl.ds(k * width, width)
        return (
            pltpu.make_async_copy(wg_hbm.at[part], wg.at[part], w_sem.at[k, 0]),
            pltpu.make_async_copy(wu_hbm.at[part], wu.at[part], w_sem.at[k, 1]),
        )

    for k in range(chunks):
        for copy in weights(k):
            copy.start()
    me, dp, chip, core = greet(experts, chips)
    sibling = 2 * chip + 1 - core

    def to_expert(k, i):
        peer = (me + i) % experts
        return remote(
            outgoing.at[k, peer], received.at[k, me], a_send.at[k, peer], a_recv.at[k, me],
            expert=peer,
        )

    def from_expert(k, i):
        peer = (me + i) % experts
        return remote(
            outgoing.at[k, peer], received.at[k, peer], a_send.at[k, peer], a_recv.at[k, peer],
            expert=peer,
        )

    def to_chip(k, i):
        other = 2 * ((chip + i) % chips) + core
        return remote(
            rows.at[k, dp], rows.at[k, dp], x_send.at[k, i], b_recv.at[k, dp], dp=other
        )

    def from_chip(k, i):
        other = 2 * ((chip + i) % chips) + core
        return remote(
            rows.at[k, other], rows.at[k, other], x_send.at[k, i], b_recv.at[k, other], dp=other
        )

    def to_sibling(k, i):
        block = 2 * ((chip + i) % chips) + core
        return remote(
            rows.at[k, block], rows.at[k, block], s_send.at[k, i], b_recv.at[k, block],
            dp=sibling,
        )

    def from_sibling(k, i):
        block = 2 * ((chip + i) % chips) + 1 - core
        return remote(
            rows.at[k, block], rows.at[k, block], s_send.at[k, i], b_recv.at[k, block],
            dp=sibling,
        )

    for k in range(chunks):
        chosen = jnp.dot(
            pick[...], normed[:, k * width : (k + 1) * width], preferred_element_type=F32
        )
        outgoing[k] = chosen.astype(BF16).reshape(experts, slots, width)

        def send(i, carry):
            to_expert(k, i).start()
            return carry

        lax.fori_loop(1, experts, send, 0)
        received[k, me] = outgoing[k, me]

    for step in range(chunks + 2):
        if step < chunks:

            def take(i, carry):
                from_expert(step, i).wait_recv()
                return carry

            lax.fori_loop(1, experts, take, 0)
            packed = jnp.dot(
                pack[...],
                received[step].reshape(experts * slots, width),
                preferred_element_type=F32,
            )
            rows[step, dp] = packed.astype(BF16)
            for i in range(1, chips):
                to_chip(step, i).start()
            to_sibling(step, 0).start()
        if 1 <= step <= chunks:
            for i in range(1, chips):
                from_chip(step - 1, i).wait_recv()
                to_sibling(step - 1, i).start()
        if step >= 2:
            k = step - 2
            for i in range(chips):
                from_sibling(k, i).wait_recv()
            for copy in weights(k):
                copy.wait()

            def multiply(n, carry):
                cols = pl.ds(pl.multiple_of(n * tile, tile), tile)
                depth = pl.ds(k * width, width)
                block = rows[k].reshape(dp_count * room, width)
                g = jnp.dot(block, wg[depth, cols], preferred_element_type=F32)
                u = jnp.dot(block, wu[depth, cols], preferred_element_type=F32)
                if k > 0:
                    g = g + acc_g[:, cols]
                    u = u + acc_u[:, cols]
                if k < chunks - 1:
                    acc_g[:, cols] = g
                    acc_u[:, cols] = u
                else:
                    hidden[:, cols] = (jax.nn.gelu(g, approximate=True) * u).astype(BF16)
                return carry

            lax.fori_loop(0, ff // tile, multiply, 0)

    for k in range(chunks):

        def sent(i, carry):
            to_expert(k, i).wait_send()
            return carry

        lax.fori_loop(1, experts, sent, 0)
        for i in range(1, chips):
            to_chip(k, i).wait_send()
        for i in range(chips):
            to_sibling(k, i).wait_send()


def kernel_out(
    experts, chips, chunks,
    hidden, unpack, mixing, wd_hbm, out,
    wd, own, sib_out, sib_in, x_out, x_in, returning, arrived, mix_high, mix_low,
    w_sem, s_send, s_recv, x_send, x_recv, a_send, a_recv,
):
    width = out.shape[1] // chunks
    slots = arrived.shape[2]

    def weights(k):
        part = pl.ds(k * width, width)
        return pltpu.make_async_copy(wd_hbm.at[:, part], wd.at[k], w_sem.at[k])

    for k in range(chunks):
        weights(k).start()
    me, dp, chip, core = greet(experts, chips)
    sibling = 2 * chip + 1 - core
    high = mixing[...].astype(BF16)
    mix_high[...] = high
    mix_low[...] = (mixing[...] - high.astype(F32)).astype(BF16)

    def sib_copy(k, i):
        return remote(
            sib_out.at[k, i], sib_in.at[k, i], s_send.at[k, i], s_recv.at[k, i], dp=sibling
        )

    def chip_copy(k, i):
        return remote(
            x_out.at[k, i - 1], x_in.at[k, i - 1], x_send.at[k, i - 1], x_recv.at[k, i - 1],
            dp=2 * ((chip + i) % chips) + core,
        )

    def to_expert(k, i):
        peer = (me + i) % experts
        return remote(
            returning.at[k, peer], arrived.at[k, me], a_send.at[k, peer], a_recv.at[k, me],
            expert=peer,
        )

    def from_expert(k, i):
        peer = (me + i) % experts
        return remote(
            returning.at[k, peer], arrived.at[k, peer], a_send.at[k, peer], a_recv.at[k, peer],
            expert=peer,
        )

    for step in range(chunks + 3):
        if step < chunks:
            k = step
            weights(k).wait()

            def give(i, carry):
                block = 2 * ((chip + i) % chips) + 1 - core
                term = jnp.dot(hidden[block], wd[k], preferred_element_type=F32)
                sib_out[k, i] = term.astype(BF16)
                sib_copy(k, i).start()
                return carry

            lax.fori_loop(0, chips, give, 0)

            def keep(i, carry):
                block = 2 * ((chip + i) % chips) + core
                own[k, i] = jnp.dot(hidden[block], wd[k], preferred_element_type=F32)
                return carry

            lax.fori_loop(0, chips, keep, 0)
        if 1 <= step <= chunks:
            k = step - 1
            for i in range(chips):
                sib_copy(k, i).wait_recv()
            for i in range(1, chips):
                x_out[k, i - 1] = (own[k, i] + sib_in[k, i].astype(F32)).astype(BF16)
                chip_copy(k, i).start()
        if 2 <= step <= chunks + 1:
            k = step - 2
            total = own[k, 0] + sib_in[k, 0].astype(F32)
            for i in range(1, chips):
                chip_copy(k, i).wait_recv()
                total = total + x_in[k, i - 1].astype(F32)
            spread = jnp.dot(unpack[...], total.astype(BF16), preferred_element_type=F32)
            returning[k] = spread.astype(BF16).reshape(experts, slots, width)

            def send(i, carry):
                to_expert(k, i).start()
                return carry

            lax.fori_loop(1, experts, send, 0)
            arrived[k, me] = returning[k, me]
        if step >= 3:
            k = step - 3

            def take(i, carry):
                from_expert(k, i).wait_recv()
                return carry

            lax.fori_loop(1, experts, take, 0)
            values = arrived[k].reshape(experts * slots, width)
            combined = jnp.dot(mix_high[...], values, preferred_element_type=F32)
            combined = combined + jnp.dot(mix_low[...], values, preferred_element_type=F32)
            out[:, k * width : (k + 1) * width] = combined.astype(BF16)

    for k in range(chunks):
        for i in range(chips):
            sib_copy(k, i).wait_send()
        for i in range(1, chips):
            chip_copy(k, i).wait_send()

        def sent(i, carry):
            to_expert(k, i).wait_send()
            return carry

        lax.fori_loop(1, experts, sent, 0)


def per_device(tokens, norm_gain, router_weight, w_gate, w_up, w_down, selected):
    dp_count = lax.axis_size("dp")
    experts = lax.axis_size("expert")
    chips = dp_count // 2
    tok_rows, model_width = tokens.shape
    capacity = selected.shape[1]
    ff = w_gate.shape[2]
    slots = 4 * tok_rows // experts
    room = 3 * capacity // (2 * dp_count)
    dp_index = lax.axis_index("dp")
    expert_index = lax.axis_index("expert")
    source = dp_index * experts + expert_index
    activations = tokens.astype(F32)
    mean_square = jnp.mean(activations * activations, axis=1, keepdims=True)
    normed = (activations * lax.rsqrt(mean_square + 1e-06) * norm_gain.astype(F32)).astype(BF16)
    gate_probs = jax.nn.sigmoid(jnp.dot(normed, router_weight, preferred_element_type=F32))

    mine = source * tok_rows + jnp.arange(tok_rows, dtype=jnp.int32)
    member = jnp.any(selected[:, :, None] == mine[None, None, :], axis=1)
    order = jnp.arange(tok_rows, dtype=jnp.int32)
    before = (order[:, None] < order[None, :]).astype(BF16)
    rank = jnp.dot(member.astype(BF16), before, preferred_element_type=F32)
    slot = jnp.arange(slots, dtype=F32)
    chosen = member[:, None, :] & (rank[:, None, :] == slot[None, :, None])
    pick = chosen.astype(BF16).reshape(experts * slots, tok_rows)
    mixing = jnp.where(chosen, gate_probs.T[:, None, :], 0.0).reshape(experts * slots, tok_rows).T

    expert_row = lax.dynamic_index_in_dim(selected, expert_index, 0, keepdims=False)
    senders = jnp.arange(experts, dtype=jnp.int32)
    first_token = (dp_index * experts + senders) * tok_rows
    firsts = jnp.sum((expert_row[None, :] < first_token[:, None]).astype(jnp.int32), axis=1)
    lasts = jnp.sum(
        (expert_row[None, :] < first_token[:, None] + tok_rows).astype(jnp.int32), axis=1
    )
    places = jnp.arange(slots, dtype=jnp.int32)
    target = jnp.where(
        places[None, :] < (lasts - firsts)[:, None],
        (firsts - firsts[0])[:, None] + places[None, :],
        -1,
    ).reshape(-1)
    spots = jnp.arange(room, dtype=jnp.int32)
    pack = (spots[:, None] == target[None, :]).astype(BF16)
    unpack = (target[:, None] == spots[None, :]).astype(BF16)

    in_vmem = pl.BlockSpec(memory_space=pltpu.VMEM)
    in_any = pl.BlockSpec(memory_space=pl.ANY)
    dma = pltpu.SemaphoreType.DMA
    all_rows = dp_count * room
    chunks = CHUNKS_IN
    width = model_width // chunks
    hidden = pl.pallas_call(
        functools.partial(kernel_in, experts, chips, chunks),
        out_shape=jax.ShapeDtypeStruct((all_rows, ff), BF16),
        in_specs=[in_vmem, in_vmem, in_vmem, in_any, in_any],
        out_specs=in_vmem,
        scratch_shapes=[
            pltpu.VMEM((chunks, experts, slots, width), BF16),
            pltpu.VMEM((chunks, experts, slots, width), BF16),
            pltpu.VMEM((chunks, dp_count, room, width), BF16),
            pltpu.VMEM((model_width, ff), BF16),
            pltpu.VMEM((model_width, ff), BF16),
            pltpu.VMEM((all_rows, ff), F32),
            pltpu.VMEM((all_rows, ff), F32),
            dma((chunks, 2)),
            dma((chunks, experts)),
            dma((chunks, experts)),
            dma((chunks, chips)),
            dma((chunks, chips)),
            dma((chunks, dp_count)),
        ],
        compiler_params=pltpu.CompilerParams(
            collective_id=0, has_side_effects=True, vmem_limit_bytes=60 * 2**20
        ),
        name="dispatch",
    )(normed, pick, pack, w_gate[0], w_up[0])

    chunks = CHUNKS_OUT
    width = model_width // chunks
    return pl.pallas_call(
        functools.partial(kernel_out, experts, chips, chunks),
        out_shape=jax.ShapeDtypeStruct((tok_rows, model_width), BF16),
        in_specs=[in_vmem, in_vmem, in_vmem, in_any],
        out_specs=in_vmem,
        scratch_shapes=[
            pltpu.VMEM((chunks, ff, width), BF16),
            pltpu.VMEM((chunks, chips, room, width), F32),
            pltpu.VMEM((chunks, chips, room, width), BF16),
            pltpu.VMEM((chunks, chips, room, width), BF16),
            pltpu.VMEM((chunks, max(chips - 1, 1), room, width), BF16),
            pltpu.VMEM((chunks, max(chips - 1, 1), room, width), BF16),
            pltpu.VMEM((chunks, experts, slots, width), BF16),
            pltpu.VMEM((chunks, experts, slots, width), BF16),
            pltpu.VMEM((tok_rows, experts * slots), BF16),
            pltpu.VMEM((tok_rows, experts * slots), BF16),
            dma((chunks,)),
            dma((chunks, chips)),
            dma((chunks, chips)),
            dma((chunks, max(chips - 1, 1))),
            dma((chunks, max(chips - 1, 1))),
            dma((chunks, experts)),
            dma((chunks, experts)),
        ],
        compiler_params=pltpu.CompilerParams(
            collective_id=1, has_side_effects=True, vmem_limit_bytes=60 * 2**20
        ),
        name="combine",
    )(hidden.reshape(dp_count, room, ff), unpack, mixing, w_down[0])


def solution(mesh):
    in_specs = (
        P(("dp", "expert"), None),
        P(),
        P(),
        P("expert", None, "dp"),
        P("expert", None, "dp"),
        P("expert", "dp", None),
        P(),
    )
    out_specs = P(("dp", "expert"), None)
    return jax.shard_map(
        per_device, mesh=mesh, in_specs=in_specs, out_specs=out_specs, check_vma=False
    )
```

time: 337 us -> 156 us (0.46)
  waiting for transfers between devices: 211 us -> 0 us
  Pallas kernels: 0 us -> 142 us
  local copies, waits for them, and re-layouts: 48 us -> 4.08 us
  matrix products: 33.1 us -> 0.37 us
  between operations: 13.6 us -> 0.12 us
  starting transfers between devices: 12.9 us -> 0 us
  other arithmetic: 17.5 us -> 8.38 us
    pallas_call x0 -> x2, Pallas kernels: none -> 142 us  [the longest x1 74.4 us: per_device(): pl.pallas_call(functools.partial(kernel_in, experts, chips, chunks), out_...]
    reduce_scatter x1 -> x0, waiting for transfers between devices: 86.7 us -> none  [per_device(): lax.psum_scatter(term_rows, 'dp', scatter_dimension=0, tiled=True)]
    all_to_all x2 -> x0, waiting for transfers between devices: 84.7 us -> none  [the longest x1 44.6 us: per_device(): lax.all_to_all(returning, 'expert', split_axis=0, concat_axis=0, tiled=True)]
    all_gather x1 -> x0, waiting for transfers between devices: 39.7 us -> none  [per_device(): everything = lax.all_gather(packed, 'dp', axis=0, tiled=True)]
    dot_general x4 -> x2, matrix products: 33.1 us -> 0.37 us  [the longest x1 0.24 us: per_device(): jnp.dot(normed, router_weight, preferred_element_type=F32)]
    gather x11 -> x0, local copies, waits for them, and re-layouts: 31.9 us -> none  [the longest x1 12.1 us: per_device(): expert_rows = everything[row_index]]
    scatter x1 -> x0, local copies, waits for them, and re-layouts: 14.2 us -> none  [per_device(): jnp.zeros((dp_count * row_room, model_width), jnp.float32).at[row_index]]
    all_to_all x2 -> x0, starting transfers between devices: 12.8 us -> none  [the longest x1 7.31 us: per_device(): lax.all_to_all(outgoing, 'expert', split_axis=0, concat_axis=0, tiled=True)]
  transfers between devices with their start and end apart: 4 -> 0, of which waited for: 4 -> 0; matrix products, arithmetic and copies ran while one was open for 4% -> 0% of each run, Pallas kernels for 0% -> 0%
where the time goes in v1:
time: 156 us; the launch traced here: 155 us
  Pallas kernels  142 us (91%)
  other arithmetic  8.38 us (5%)
  local copies, waits for them, and re-layouts  4.08 us (3%)
    pallas_call x1, Pallas kernels, per_device(): pl.pallas_call(functools.partial(kernel_in, experts, chips, chunks), out_...  74.4 us
    pallas_call x1, Pallas kernels, per_device(): pl.pallas_call(functools.partial(kernel_out, experts, chips, chunks), out...  67.6 us

profile of v1, /device:TPU:0, one launch (start us, length us, event | category | flops | bytes accessed | tf_op | source)
XLA Modules:
  0.0 155.0 jit_solution(13771543428787712802)
XLA Ops:
  0.0 0.0 copy-start
  0.0 0.8 dynamic-slice_reduce_fusion
  0.8 0.2 convert_reduce_fusion.1
  1.0 0.1 fusion.10
  1.1 0.1 add_select_fusion
  1.1 0.1 select_n.26
  1.2 0.8 fusion.8.pack
  2.0 2.4 %compare_reduce_fusion = pred[8,128]{1,0:T(8,128)(4,1)S(1)} fusion(s32[128]{0:T(128)S(1)} %iota_add_fusion, s32[8,896]{1,0:T(8,128)} %param.13), kind=kLoop, calls=%fused_computation | loop fusion | flops 1833984 | bytes 30208 | tf_op jit(solution)/shard_map/reduce_or | solution.py:332
  4.4 0.1 fusion.9
  4.6 0.1 copy.15
  4.8 0.2 copy.16
  4.9 0.7 convert_element_type.28
  5.6 1.2 fusion.4
  6.8 1.2 fusion.6.normed
  8.1 0.0 copy-done
  8.1 0.0 copy-start.1
  8.1 0.2 fusion.3
  8.4 0.1 copy.18
  8.5 0.1 eq.66
  8.6 0.8 select_bitcast_fusion
  9.4 0.8 copy.17.pick
  10.2 0.0 copy-done.1
  10.2 74.4 %dispatch.1 = bf16[1344,1280]{1,0:T(8,128)(2,1)} custom-call(bf16[128,2048]{1,0:T(8,128)(2,1)} %copy-done.1, bf16[512,128]{1,0:T(8,128)(2,1)} %copy.17.pick, bf16[336,512]{1,0:T(8,128)(2,1)} %fusion.8.pack, bf16[2048,1280]{1,0:T(8,128)(2,1)} %bitcast.17, bf16[2048,1280]{1,0:T(8,128)(2,1)} %bitcast.18), custom_call_target="tpu_custom_call" | custom-call | tf_op jit(solution)/shard_map/dispatch/pallas_call | solution.py:364
  84.6 0.9 fusion.7.unpack
  85.5 67.6 %combine.1 = bf16[128,2048]{1,0:T(8,128)(2,1)} custom-call(bf16[4,336,1280]{2,1,0:T(8,128)(2,1)} %bitcast.16, bf16[512,336]{1,0:T(8,128)(2,1)} %fusion.7.unpack, f32[128,512]{1,0:T(8,128)} %get-tuple-element.7.mixing, bf16[1280,2048]{1,0:T(8,128)(2,1)} %bitcast.19), custom_call_target="tpu_custom_call" | custom-call | tf_op jit(solution)/shard_map/combine/pallas_call | solution.py:392
  153.2 1.9 %copy.20 = bf16[128,2048]{1,0:T(8,128)(2,1)} copy(bf16[128,2048]{1,0:T(8,128)(2,1)} %combine.1) | data formatting | bytes 1048576
  (8 shorter events, 0.1 us)
Async XLA Ops:
  0.0 8.1 %copy-start = (bf16[2048,8]{0,1:T(8,128)(2,1)S(1)}, bf16[2048,8]{0,1:T(8,128)(2,1)}, u32[]{:S(2)}) copy-start(bf16[2048,8]{0,1:T(8,128)(2,1)} %param.9) | copy-start | bytes 98308
  8.1 2.1 %copy-start.1 = (bf16[128,2048]{1,0:T(8,128)(2,1)}, bf16[128,2048]{1,0:T(8,128)(2,1)S(1)}, u32[]{:S(2)}) copy-start(bf16[128,2048]{1,0:T(8,128)(2,1)S(1)} %fusion.6.normed) | copy-start | bytes 1572868

commit v2 on v1

--- a/solution.py
+++ b/solution.py
@@ -10,8 +10,9 @@
 MESH = pl.DeviceIdType.MESH
 F32 = jnp.float32
 BF16 = jnp.bfloat16
-CHUNKS_IN = 4
-CHUNKS_OUT = 4
+CHUNKS_IN = 8
+CHUNKS_OUT = 8
+AHEAD = 2
 
 
 def tile_of(width):
@@ -27,13 +28,19 @@
     chip, core = dp // 2, dp % 2
     barrier = pltpu.get_barrier_semaphore()
 
+    half = experts // 2
+    base, local = (me // half) * half, me % half
+
     def expert_hello(i, carry):
         pl.semaphore_signal(
-            barrier, inc=1, device_id={"expert": (me + i) % experts}, device_id_type=MESH
+            barrier, inc=1, device_id={"expert": base + (local + i) % half}, device_id_type=MESH
         )
         return carry
 
-    lax.fori_loop(1, experts, expert_hello, 0)
+    lax.fori_loop(1, half, expert_hello, 0)
+    pl.semaphore_signal(
+        barrier, inc=1, device_id={"expert": (me + half) % experts}, device_id_type=MESH
+    )
     pl.semaphore_signal(
         barrier, inc=1, device_id={"dp": 2 * chip + 1 - core}, device_id_type=MESH
     )
@@ -44,7 +51,7 @@
             device_id={"dp": 2 * ((chip + i) % chips) + core},
             device_id_type=MESH,
         )
-    pl.semaphore_wait(barrier, experts - 1 + chips)
+    pl.semaphore_wait(barrier, half + chips)
     return me, dp, chip, core
 
 
@@ -62,12 +69,13 @@
 def kernel_in(
     experts, chips, chunks,
     normed, pick, pack, wg_hbm, wu_hbm, hidden,
-    outgoing, received, rows, wg, wu, acc_g, acc_u,
-    w_sem, a_send, a_recv, x_send, s_send, b_recv,
+    tok_out, tok_in, outgoing, received, rows, wg, wu, acc_g, acc_u,
+    w_sem, t_send, t_recv, a_send, a_recv, x_send, s_send, b_recv,
 ):
+    half = experts // 2
     dp_count = 2 * chips
     width = normed.shape[1] // chunks
-    slots = outgoing.shape[2]
+    slots = received.shape[2]
     room = rows.shape[2]
     ff = wg.shape[1]
     tile = tile_of(ff)
@@ -80,87 +88,109 @@
         )
 
     for k in range(chunks):
+        tok_out[k] = normed[:, k * width : (k + 1) * width]
+    me, dp, chip, core = greet(experts, chips)
+    base, local = (me // half) * half, me % half
+    partner = (me + half) % experts
+    sibling = 2 * chip + 1 - core
+
+    def to_partner(k):
+        return remote(
+            tok_out.at[k], tok_in.at[k], t_send.at[k], t_recv.at[k], expert=partner
+        )
+
+    def to_expert(k, side, i):
+        near = (local + i) % half
+        owner = (me + side * half) % experts
+        return remote(
+            outgoing.at[k, side, near], received.at[k, owner],
+            a_send.at[k, side, near], a_recv.at[k, owner], expert=base + near,
+        )
+
+    def from_expert(k, side, i):
+        near = (local + i) % half
+        owner = (base + near + side * half) % experts
+        return remote(
+            outgoing.at[k, side, near], received.at[k, owner],
+            a_send.at[k, side, near], a_recv.at[k, owner], expert=base + near,
+        )
+
+    def to_chip(k, i):
+        other = 2 * ((chip + i) % chips) + core
+        return remote(
+            rows.at[k, dp], rows.at[k, dp], x_send.at[k, i], b_recv.at[k, dp], dp=other
+        )
+
+    def from_chip(k, i):
+        other = 2 * ((chip + i) % chips) + core
+        return remote(
+            rows.at[k, other], rows.at[k, other], x_send.at[k, i], b_recv.at[k, other], dp=other
+        )
+
+    def to_sibling(k, i):
+        block = 2 * ((chip + i) % chips) + core
+        return remote(
+            rows.at[k, block], rows.at[k, block], s_send.at[k, i], b_recv.at[k, block],
+            dp=sibling,
+        )
+
+    def from_sibling(k, i):
+        block = 2 * ((chip + i) % chips) + 1 - core
+        return remote(
+            rows.at[k, block], rows.at[k, block], s_send.at[k, i], b_recv.at[k, block],
+            dp=sibling,
+        )
+
+    def send_rows(k, side, source):
+        chosen = jnp.dot(pick[side], source, preferred_element_type=F32)
+        outgoing[k, side] = chosen.astype(BF16).reshape(half, slots, width)
+
+        def send(i, carry):
+            to_expert(k, side, i).start()
+            return carry
+
+        lax.fori_loop(1, half, send, 0)
+        received[k, (me + side * half) % experts] = outgoing[k, side, local]
+
+    for k in range(min(AHEAD, chunks)):
+        to_partner(k).start()
+    send_rows(0, 0, tok_out[0])
+    for k in range(chunks):
         for copy in weights(k):
             copy.start()
-    me, dp, chip, core = greet(experts, chips)
-    sibling = 2 * chip + 1 - core
-
-    def to_expert(k, i):
-        peer = (me + i) % experts
-        return remote(
-            outgoing.at[k, peer], received.at[k, me], a_send.at[k, peer], a_recv.at[k, me],
-            expert=peer,
-        )
-
-    def from_expert(k, i):
-        peer = (me + i) % experts
-        return remote(
-            outgoing.at[k, peer], received.at[k, peer], a_send.at[k, peer], a_recv.at[k, peer],
-            expert=peer,
-        )
-
-    def to_chip(k, i):
-        other = 2 * ((chip + i) % chips) + core
-        return remote(
-            rows.at[k, dp], rows.at[k, dp], x_send.at[k, i], b_recv.at[k, dp], dp=other
-        )
-
-    def from_chip(k, i):
-        other = 2 * ((chip + i) % chips) + core
-        return remote(
-            rows.at[k, other], rows.at[k, other], x_send.at[k, i], b_recv.at[k, other], dp=other
-        )
-
-    def to_sibling(k, i):
-        block = 2 * ((chip + i) % chips) + core
-        return remote(
-            rows.at[k, block], rows.at[k, block], s_send.at[k, i], b_recv.at[k, block],
-            dp=sibling,
-        )
-
-    def from_sibling(k, i):
-        block = 2 * ((chip + i) % chips) + 1 - core
-        return remote(
-            rows.at[k, block], rows.at[k, block], s_send.at[k, i], b_recv.at[k, block],
-            dp=sibling,
-        )
-
-    for k in range(chunks):
-        chosen = jnp.dot(
-            pick[...], normed[:, k * width : (k + 1) * width], preferred_element_type=F32
-        )
-        outgoing[k] = chosen.astype(BF16).reshape(experts, slots, width)
-
-        def send(i, carry):
-            to_expert(k, i).start()
-            return carry
-
-        lax.fori_loop(1, experts, send, 0)
-        received[k, me] = outgoing[k, me]
-
-    for step in range(chunks + 2):
+
+    for step in range(chunks + 3):
+        if step + AHEAD < chunks:
+            to_partner(step + AHEAD).start()
+        if step + 1 < chunks:
+            send_rows(step + 1, 0, tok_out[step + 1])
         if step < chunks:
+            to_partner(step).wait_recv()
+            send_rows(step, 1, tok_in[step])
+        if 1 <= step <= chunks:
+            k = step - 1
 
             def take(i, carry):
-                from_expert(step, i).wait_recv()
+                from_expert(k, 0, i).wait_recv()
+                from_expert(k, 1, i).wait_recv()
                 return carry
 
-            lax.fori_loop(1, experts, take, 0)
+            lax.fori_loop(1, half, take, 0)
             packed = jnp.dot(
                 pack[...],
-                received[step].reshape(experts * slots, width),
+                received[k].reshape(experts * slots, width),
                 preferred_element_type=F32,
             )
-            rows[step, dp] = packed.astype(BF16)
+            rows[k, dp] = packed.astype(BF16)
             for i in range(1, chips):
-                to_chip(step, i).start()
-            to_sibling(step, 0).start()
-        if 1 <= step <= chunks:
+                to_chip(k, i).start()
+            to_sibling(k, 0).start()
+        if 2 <= step <= chunks + 1:
             for i in range(1, chips):
-                from_chip(step - 1, i).wait_recv()
-                to_sibling(step - 1, i).start()
-        if step >= 2:
-            k = step - 2
+                from_chip(step - 2, i).wait_recv()
+                to_sibling(step - 2, i).start()
+        if step >= 3:
+            k = step - 3
             for i in range(chips):
                 from_sibling(k, i).wait_recv()
             for copy in weights(k):
@@ -185,12 +215,14 @@
             lax.fori_loop(0, ff // tile, multiply, 0)
 
     for k in range(chunks):
+        to_partner(k).wait_send()
 
         def sent(i, carry):
-            to_expert(k, i).wait_send()
+            to_expert(k, 0, i).wait_send()
+            to_expert(k, 1, i).wait_send()
             return carry
 
-        lax.fori_loop(1, experts, sent, 0)
+        lax.fori_loop(1, half, sent, 0)
         for i in range(1, chips):
             to_chip(k, i).wait_send()
         for i in range(chips):
@@ -200,11 +232,13 @@
 def kernel_out(
     experts, chips, chunks,
     hidden, unpack, mixing, wd_hbm, out,
-    wd, own, sib_out, sib_in, x_out, x_in, returning, arrived, mix_high, mix_low,
-    w_sem, s_send, s_recv, x_send, x_recv, a_send, a_recv,
+    wd, own, sib_out, sib_in, x_out, x_in, returning, arrived, tok_out, tok_in,
+    mix_high, mix_low,
+    w_sem, s_send, s_recv, x_send, x_recv, a_send, a_recv, t_send, t_recv,
 ):
+    half = experts // 2
     width = out.shape[1] // chunks
-    slots = arrived.shape[2]
+    slots = arrived.shape[3]
 
     def weights(k):
         part = pl.ds(k * width, width)
@@ -213,6 +247,8 @@
     for k in range(chunks):
         weights(k).start()
     me, dp, chip, core = greet(experts, chips)
+    base, local = (me // half) * half, me % half
+    partner = (me + half) % experts
     sibling = 2 * chip + 1 - core
     high = mixing[...].astype(BF16)
     mix_high[...] = high
@@ -229,21 +265,40 @@
             dp=2 * ((chip + i) % chips) + core,
         )
 
-    def to_expert(k, i):
-        peer = (me + i) % experts
-        return remote(
-            returning.at[k, peer], arrived.at[k, me], a_send.at[k, peer], a_recv.at[k, me],
-            expert=peer,
-        )
-
-    def from_expert(k, i):
-        peer = (me + i) % experts
-        return remote(
-            returning.at[k, peer], arrived.at[k, peer], a_send.at[k, peer], a_recv.at[k, peer],
-            expert=peer,
-        )
-
-    for step in range(chunks + 3):
+    def to_expert(k, side, i):
+        near = (local + i) % half
+        owner = (base + near + side * half) % experts
+        return remote(
+            returning.at[k, owner], arrived.at[k, side, local],
+            a_send.at[k, owner], a_recv.at[k, side, local], expert=base + near,
+        )
+
+    def from_expert(k, side, i):
+        near = (local + i) % half
+        owner = (base + near + side * half) % experts
+        return remote(
+            returning.at[k, owner], arrived.at[k, side, near],
+            a_send.at[k, owner], a_recv.at[k, side, near], expert=base + near,
+        )
+
+    def to_partner(k):
+        return remote(
+            tok_out.at[k], tok_in.at[k], t_send.at[k], t_recv.at[k], expert=partner
+        )
+
+    def mixed(k, side):
+        values = arrived[k, side].reshape(half * slots, width)
+        sums = jnp.dot(mix_high[side], values, preferred_element_type=F32)
+        return sums + jnp.dot(mix_low[side], values, preferred_element_type=F32)
+
+    def take_side(k, side):
+        def take(i, carry):
+            from_expert(k, side, i).wait_recv()
+            return carry
+
+        lax.fori_loop(1, half, take, 0)
+
+    for step in range(chunks + 4):
         if step < chunks:
             k = step
             weights(k).wait()
@@ -278,24 +333,25 @@
                 total = total + x_in[k, i - 1].astype(F32)
             spread = jnp.dot(unpack[...], total.astype(BF16), preferred_element_type=F32)
             returning[k] = spread.astype(BF16).reshape(experts, slots, width)
-
-            def send(i, carry):
-                to_expert(k, i).start()
-                return carry
-
-            lax.fori_loop(1, experts, send, 0)
-            arrived[k, me] = returning[k, me]
-        if step >= 3:
+            for side in (1, 0):
+
+                def send(i, carry):
+                    to_expert(k, side, i).start()
+                    return carry
+
+                lax.fori_loop(1, half, send, 0)
+                arrived[k, side, local] = returning[k, (me + side * half) % experts]
+        if 3 <= step <= chunks + 2:
             k = step - 3
-
-            def take(i, carry):
-                from_expert(k, i).wait_recv()
-                return carry
-
-            lax.fori_loop(1, experts, take, 0)
-            values = arrived[k].reshape(experts * slots, width)
-            combined = jnp.dot(mix_high[...], values, preferred_element_type=F32)
-            combined = combined + jnp.dot(mix_low[...], values, preferred_element_type=F32)
+            take_side(k, 1)
+            tok_out[k] = mixed(k, 1).astype(BF16)
+            to_partner(k).start()
+        if step >= 4:
+            k = step - 4
+            take_side(k, 0)
+            near_sum = mixed(k, 0)
+            to_partner(k).wait_recv()
+            combined = near_sum + tok_in[k].astype(F32)
             out[:, k * width : (k + 1) * width] = combined.astype(BF16)
 
     for k in range(chunks):
@@ -303,12 +359,14 @@
             sib_copy(k, i).wait_send()
         for i in range(1, chips):
             chip_copy(k, i).wait_send()
+        to_partner(k).wait_send()
 
         def sent(i, carry):
-            to_expert(k, i).wait_send()
+            to_expert(k, 0, i).wait_send()
+            to_expert(k, 1, i).wait_send()
             return carry
 
-        lax.fori_loop(1, experts, sent, 0)
+        lax.fori_loop(1, half, sent, 0)
 
 
 def per_device(tokens, norm_gain, router_weight, w_gate, w_up, w_down, selected):
@@ -322,21 +380,33 @@
     room = 3 * capacity // (2 * dp_count)
     dp_index = lax.axis_index("dp")
     expert_index = lax.axis_index("expert")
-    source = dp_index * experts + expert_index
     activations = tokens.astype(F32)
     mean_square = jnp.mean(activations * activations, axis=1, keepdims=True)
     normed = (activations * lax.rsqrt(mean_square + 1e-06) * norm_gain.astype(F32)).astype(BF16)
     gate_probs = jax.nn.sigmoid(jnp.dot(normed, router_weight, preferred_element_type=F32))
 
-    mine = source * tok_rows + jnp.arange(tok_rows, dtype=jnp.int32)
-    member = jnp.any(selected[:, :, None] == mine[None, None, :], axis=1)
+    half = experts // 2
+    base = (expert_index // half) * half
+    partner = (expert_index + half) % experts
+    near = lax.dynamic_slice_in_dim(selected, base, half, 0)
+    pair = dp_index * experts + jnp.stack([expert_index, partner])
     order = jnp.arange(tok_rows, dtype=jnp.int32)
+    ours = (pair[:, None] * tok_rows + order[None, :]).reshape(-1)
+    member = jnp.any(near[:, :, None] == ours[None, None, :], axis=1)
+    member = member.reshape(half * 2, tok_rows)
     before = (order[:, None] < order[None, :]).astype(BF16)
     rank = jnp.dot(member.astype(BF16), before, preferred_element_type=F32)
     slot = jnp.arange(slots, dtype=F32)
-    chosen = member[:, None, :] & (rank[:, None, :] == slot[None, :, None])
-    pick = chosen.astype(BF16).reshape(experts * slots, tok_rows)
-    mixing = jnp.where(chosen, gate_probs.T[:, None, :], 0.0).reshape(experts * slots, tok_rows).T
+    place = jnp.where(member, rank, -1.0).reshape(half, 2, tok_rows).transpose(1, 0, 2)
+    chosen = place[:, :, None, :] == slot[None, None, :, None]
+    pick = chosen.astype(BF16).reshape(2, half * slots, tok_rows)
+    swap = [(e, (e + half) % experts) for e in range(experts)]
+    far_probs = lax.ppermute(gate_probs, "expert", swap)
+    probs = lax.dynamic_slice_in_dim(jnp.stack([gate_probs, far_probs]), base, half, 2)
+    placed = place.transpose(0, 2, 1)
+    mixing = jnp.where(
+        placed[:, :, :, None] == slot[None, None, None, :], probs[:, :, :, None], 0.0
+    ).reshape(2, tok_rows, half * slots)
 
     expert_row = lax.dynamic_index_in_dim(selected, expert_index, 0, keepdims=False)
     senders = jnp.arange(experts, dtype=jnp.int32)
@@ -367,7 +437,9 @@
         in_specs=[in_vmem, in_vmem, in_vmem, in_any, in_any],
         out_specs=in_vmem,
         scratch_shapes=[
-            pltpu.VMEM((chunks, experts, slots, width), BF16),
+            pltpu.VMEM((chunks, tok_rows, width), BF16),
+            pltpu.VMEM((chunks, tok_rows, width), BF16),
+            pltpu.VMEM((chunks, 2, half, slots, width), BF16),
             pltpu.VMEM((chunks, experts, slots, width), BF16),
             pltpu.VMEM((chunks, dp_count, room, width), BF16),
             pltpu.VMEM((model_width, ff), BF16),
@@ -375,7 +447,9 @@
             pltpu.VMEM((all_rows, ff), F32),
             pltpu.VMEM((all_rows, ff), F32),
             dma((chunks, 2)),
-            dma((chunks, experts)),
+            dma((chunks,)),
+            dma((chunks,)),
+            dma((chunks, 2, half)),
             dma((chunks, experts)),
             dma((chunks, chips)),
             dma((chunks, chips)),
@@ -402,16 +476,20 @@
             pltpu.VMEM((chunks, max(chips - 1, 1), room, width), BF16),
             pltpu.VMEM((chunks, max(chips - 1, 1), room, width), BF16),
             pltpu.VMEM((chunks, experts, slots, width), BF16),
-            pltpu.VMEM((chunks, experts, slots, width), BF16),
-            pltpu.VMEM((tok_rows, experts * slots), BF16),
-            pltpu.VMEM((tok_rows, experts * slots), BF16),
+            pltpu.VMEM((chunks, 2, half, slots, width), BF16),
+            pltpu.VMEM((chunks, tok_rows, width), BF16),
+            pltpu.VMEM((chunks, tok_rows, width), BF16),
+            pltpu.VMEM((2, tok_rows, half * slots), BF16),
+            pltpu.VMEM((2, tok_rows, half * slots), BF16),
             dma((chunks,)),
             dma((chunks, chips)),
             dma((chunks, chips)),
             dma((chunks, max(chips - 1, 1))),
             dma((chunks, max(chips - 1, 1))),
             dma((chunks, experts)),
-            dma((chunks, experts)),
+            dma((chunks, 2, half)),
+            dma((chunks,)),
+            dma((chunks,)),
         ],
         compiler_params=pltpu.CompilerParams(
             collective_id=1, has_side_effects=True, vmem_limit_bytes=60 * 2**20

time: 156 us -> 136 us (0.87)
  Pallas kernels: 142 us -> 120 us
  starting transfers between devices: 0 us -> 4.09 us
    pallas_call x1, Pallas kernels: 74.4 us -> 62.6 us  [per_device(): pl.pallas_call(functools.partial(kernel_in, experts, chips, chunks), out_...]
    pallas_call x1, Pallas kernels: 67.6 us -> 56.9 us  [per_device(): pl.pallas_call(functools.partial(kernel_out, experts, chips, chunks), out...]
    ppermute x0 -> x1, starting transfers between devices: none -> 4.09 us  [per_device(): far_probs = lax.ppermute(gate_probs, 'expert', swap)]
    reduce_or x1, other arithmetic: 2.38 us -> 0.64 us  [per_device(): member = jnp.any(near[:, :, None] == ours[None, None, :], axis=1)]
  transfers between devices with their start and end apart: 0 -> 1, of which waited for: 0 -> 0; matrix products, arithmetic and copies ran while one was open for 0% -> 4% of each run, Pallas kernels for 0% -> 46%
where the time goes in v2:
time: 136 us; the launch traced here: 135 us
  Pallas kernels  120 us (88%)
  other arithmetic  7.5 us (6%)
  starting transfers between devices  4.09 us (3%)
  local copies, waits for them, and re-layouts  3.9 us (3%)
    pallas_call x1, Pallas kernels, per_device(): pl.pallas_call(functools.partial(kernel_in, experts, chips, chunks), out_...  62.6 us
    pallas_call x1, Pallas kernels, per_device(): pl.pallas_call(functools.partial(kernel_out, experts, chips, chunks), out...  56.9 us
    ppermute x1, starting transfers between devices, per_device(): far_probs = lax.ppermute(gate_probs, 'expert', swap)  4.09 us
  transfers between devices with their start and end apart: 1, of which 0 were waited for; matrix products, arithmetic and copies ran while one was open for 4% of the time, Pallas kernels for 46%

profile of v2, /device:TPU:0, one launch (start us, length us, event | category | flops | bytes accessed | tf_op | source)
XLA Modules:
  0.0 135.5 jit_solution(786902803163369527)
XLA Ops:
  0.0 0.0 copy-start
  0.0 0.7 convert_element_type.28
  0.7 1.2 fusion.3
  1.9 1.2 fusion.5.normed
  3.2 0.0 copy-done
  3.2 0.0 copy-start.1
  3.2 0.2 fusion.2
  3.4 4.1 %collective-permute-start = (f32[128,8]{0,1:T(8,128)S(1)}, f32[128,8]{0,1:T(8,128)S(1)}, u32[]{:S(2)}, u32[]{:S(2)}) collective-permute-start(f32[128,8]{0,1:T(8,128)S(1)} %fusion.2), channel_id=1, source_target_pairs={{0,4},{1,5},{2,6},{3,7},{4,0},{5,1},{6,2},{7,3},{8,12},{9,13},{10,... | collective-permute-start | bytes 12296 | tf_op jit(solution)/shard_map/ppermute | solution.py:404
  7.5 0.8 dynamic-slice_reduce_fusion
  8.3 0.2 convert_reduce_fusion.1
  8.5 0.1 fusion.11
  8.6 0.1 add_select_fusion
  8.7 0.1 select_n.49
  8.7 0.8 fusion.7.pack
  9.5 0.9 fusion.6.unpack
  10.4 0.8 constant_dynamic-slice_fusion
  11.2 0.1 fusion.10
  11.3 0.1 add_bitcast_fusion
  11.3 0.6 compare_reduce_fusion
  12.0 0.1 convolution_select_fusion
  12.1 0.1 eq.87
  12.3 0.1 copy.17
  12.4 0.8 fusion.8.pick
  13.2 0.0 copy-done.1
  13.2 62.6 %dispatch.1 = bf16[1344,1280]{1,0:T(8,128)(2,1)} custom-call(bf16[128,2048]{1,0:T(8,128)(2,1)} %copy-done.1, bf16[2,256,128]{2,1,0:T(8,128)(2,1)} %fusion.8.pick, bf16[336,512]{1,0:T(8,128)(2,1)} %fusion.7.pack, bf16[2048,1280]{1,0:T(8,128)(2,1)} %bitcast.27, bf16[2048,1280]{1,0:T(8,128)(2,1)} %bitcast.28), custom_call_target="tpu_custom_call" | custom-call | tf_op jit(solution)/shard_map/dispatch/pallas_call | solution.py:434
  75.8 0.0 collective-permute-done
  75.8 0.1 copy.18
  76.0 0.7 compare_select_fusion.mixing
  76.7 56.9 %combine.1 = bf16[128,2048]{1,0:T(8,128)(2,1)} custom-call(bf16[4,336,1280]{2,1,0:T(8,128)(2,1)} %bitcast.26, bf16[512,336]{1,0:T(8,128)(2,1)} %fusion.6.unpack, f32[2,128,256]{2,1,0:T(8,128)} %compare_select_fusion.mixing, bf16[1280,2048]{1,0:T(8,128)(2,1)} %bitcast.29), custom_call_target="tpu_custom_call" | custom-call | tf_op jit(solution)/shard_map/combine/pallas_call | solution.py:466
  133.6 1.9 %copy.20 = bf16[128,2048]{1,0:T(8,128)(2,1)} copy(bf16[128,2048]{1,0:T(8,128)(2,1)} %combine.1) | data formatting | bytes 1048576
  (9 shorter events, 0.1 us)
Async XLA Ops:
  0.0 3.2 %copy-start = (bf16[2048,8]{0,1:T(8,128)(2,1)S(1)}, bf16[2048,8]{0,1:T(8,128)(2,1)}, u32[]{:S(2)}) copy-start(bf16[2048,8]{0,1:T(8,128)(2,1)} %param.9) | copy-start | bytes 98308
  3.2 10.0 %copy-start.1 = (bf16[128,2048]{1,0:T(8,128)(2,1)}, bf16[128,2048]{1,0:T(8,128)(2,1)S(1)}, u32[]{:S(2)}) copy-start(bf16[128,2048]{1,0:T(8,128)(2,1)S(1)} %fusion.5.normed) | copy-start | bytes 1572868
  3.4 72.4 %collective-permute-start = (f32[128,8]{0,1:T(8,128)S(1)}, f32[128,8]{0,1:T(8,128)S(1)}, u32[]{:S(2)}, u32[]{:S(2)}) collective-permute-start(f32[128,8]{0,1:T(8,128)S(1)} %fusion.2), channel_id=1, source_target_pairs={{0,4},{1,5},{2,6},{3,7},{4,0},{5,1},{6,2},{7,3},{8,12},{9,13},{10,... | collective-permute-start | bytes 12296 | tf_op jit(solution)/shard_map/ppermute | solution.py:404
